TPU v7x, 32 devices: a whole 2x2x4 slice. The times are simulated.
32 devices in a mesh: dp: 4 (over y, core), head: 2 (over x), kv: 4 (over z).
Axes of the slice: x: 2, y: 2, z: 4, core: 2. Of those that a mesh axis runs over, the one named last changes fastest.
Arguments:
- teacher_query: bfloat16 [4, 1024, 3584], P('dp', 'kv', 'head'), may hold values from -96 to 96
- teacher_key: bfloat16 [4, 1024, 512], P('dp', 'kv', 'head'), may hold values from -8 to 8
- student_query: bfloat16 [4, 1024, 1792], P('dp', 'kv', 'head'), may hold values from -96 to 96
- student_key: bfloat16 [4, 1024, 256], P('dp', 'kv', 'head'), may hold values from -8 to 8
- pair_table: int32 [14, 2], replicated, may hold values from 0 to 27, as said below
Outputs:
- kl: float32 [4, 14, 1024], P('dp', 'head', 'kv')
- head_loss: float32 [14], P('head')
Inputs may be any that keep to these rules, and one draw needn't show every extreme that they name: `pair_table`: each of the 28 teacher heads appears exactly once in the table.
All inputs are finite; a program needn't handle non-finite values.
Results may differ from a plain program's by a relative error of at most 0.0003.
Values may be sent and summed in bfloat16 or wider, within the bound.
A program may use at most 64 MiB of HBM per device.

v0:
```python
import math
import jax
import jax.numpy as jnp
from jax import lax
from jax.sharding import PartitionSpec as P

HT = 28
KVT = 4
DH = 128
HS = 14
KVS = 2
masked_value = -1e30


def running_softmax(running_max, running_total, logits, causal_mask):
    filled = jnp.where(causal_mask, logits, masked_value)
    new_max = jnp.maximum(running_max, jnp.max(filled, axis=-1))
    rescale = jnp.exp(running_max - new_max)
    weights = jnp.where(causal_mask, jnp.exp(filled - new_max[..., None]), 0.0)
    return (new_max, running_total * rescale + jnp.sum(weights, axis=-1), rescale, weights)


def make_fold(teacher_heads, teacher_select, student_heads, student_select, repeat, query_pos):
    seq_dev, row_count, pair_count, head_dim = teacher_heads.shape
    student_count = student_heads.shape[2]
    scale = 1.0 / math.sqrt(head_dim)
    last_query = query_pos[row_count - 1]

    def fold_step(carry, pieces, start):
        teacher_keys, student_keys = pieces
        key_count = teacher_keys.shape[1]
        block_size = math.gcd(key_count, 512)
        block_total = key_count // block_size
        visible = jnp.clip(last_query // block_size + 1, 0, block_total)

        def one_block(block_index, state):
            t_max, t_total, t_cross, s_max, s_total = state
            offset = block_index * block_size
            t_block = lax.dynamic_slice_in_dim(teacher_keys, offset, block_size, 1).reshape(
                seq_dev, block_size, -1, head_dim
            )
            s_block = lax.dynamic_slice_in_dim(student_keys, offset, block_size, 1).reshape(
                seq_dev, block_size, -1, head_dim
            )
            t_keys = jnp.take(t_block, teacher_select, axis=2)
            s_keys = jnp.take(s_block, student_select, axis=2)
            t_logits = (
                jnp.einsum(
                    "bqpd,bkpd->bpqk", teacher_heads, t_keys, preferred_element_type=jnp.float32
                )
                * scale
            )
            s_logits = (
                jnp.einsum(
                    "bqsd,bksd->bsqk", student_heads, s_keys, preferred_element_type=jnp.float32
                )
                * scale
            )
            key_pos = offset + jnp.arange(block_size, dtype=jnp.int32)
            causal_mask = key_pos[None, :] <= query_pos[:, None]
            t_max, t_total, t_rescale, t_weights = running_softmax(
                t_max, t_total, t_logits, causal_mask
            )
            s_max, s_total, s_rescale, s_weights = running_softmax(
                s_max, s_total, s_logits, causal_mask
            )
            split_logits = t_logits.reshape(seq_dev, student_count, repeat, row_count, block_size)
            gap = (split_logits - s_logits[:, :, None]).reshape(
                seq_dev, pair_count, row_count, block_size
            )
            t_cross = t_cross * t_rescale + jnp.sum(t_weights * gap, axis=-1)
            return (t_max, t_total, t_cross, s_max, s_total)

        return lax.fori_loop(0, visible, one_block, carry)

    pair_shape = (seq_dev, pair_count, row_count)
    student_shape = (seq_dev, student_count, row_count)
    initial = (
        jnp.full(pair_shape, masked_value, jnp.float32),
        jnp.zeros(pair_shape, jnp.float32),
        jnp.zeros(pair_shape, jnp.float32),
        jnp.full(student_shape, masked_value, jnp.float32),
        jnp.zeros(student_shape, jnp.float32),
    )
    return (fold_step, initial)


def finish_pairs(state, repeat):
    t_max, t_total, t_cross, s_max, s_total = state
    seq_dev, pair_count, row_count = t_max.shape
    student_count = s_max.shape[1]
    t_lse = t_max + jnp.log(t_total)
    s_lse = s_max + jnp.log(s_total)
    s_paired = jnp.broadcast_to(
        s_lse[:, :, None], (seq_dev, student_count, repeat, row_count)
    ).reshape(seq_dev, pair_count, row_count)
    return t_cross / t_total - t_lse + s_paired


def per_device(teacher_query, teacher_key, student_query, student_key, pair_table):
    seq_dev, row_count, teacher_width = teacher_query.shape
    n_head = lax.axis_size("head")
    n_kv = lax.axis_size("kv")
    n_data = lax.axis_size("dp")
    head_index = lax.axis_index("head")
    kv_index = lax.axis_index("kv")
    group_teacher = HT // KVT
    group_student = HS // KVS
    local_student = HS // n_head
    local_student_kv = KVS // n_head
    query_pos = kv_index * row_count + jnp.arange(row_count, dtype=jnp.int32)
    all_tq, all_tk = (
        lax.all_gather(teacher_query, "head", axis=2, tiled=True),
        lax.all_gather(teacher_key, "head", axis=2, tiled=True),
    )
    my_pairs = lax.dynamic_slice_in_dim(
        pair_table, head_index * local_student, local_student, 0
    ).reshape(-1)
    teacher_heads = jnp.take(all_tq.reshape(seq_dev, row_count, HT, DH), my_pairs, axis=2)
    teacher_select = my_pairs // group_teacher
    student_heads = student_query.reshape(seq_dev, row_count, local_student, DH)
    student_ids = head_index * local_student + jnp.arange(local_student, dtype=jnp.int32)
    student_select = student_ids // group_student - head_index * local_student_kv
    fold_step, initial = make_fold(
        teacher_heads, teacher_select, student_heads, student_select, 2, query_pos
    )
    state = fold_step(
        initial,
        (
            lax.all_gather(all_tk, "kv", axis=1, tiled=True),
            lax.all_gather(student_key, "kv", axis=1, tiled=True),
        ),
        jnp.int32(0),
    )
    pair_kl = finish_pairs(state, 2)
    kl_local = jnp.sum(pair_kl.reshape(seq_dev, local_student, 2, row_count), axis=2)
    head_sums = jnp.sum(kl_local, axis=(0, 2))
    total = lax.psum(head_sums, ("dp", "kv"))
    head_loss = total / (seq_dev * n_data * row_count * n_kv)
    return (kl_local, head_loss)


def solution(mesh):
    in_specs = (
        P("dp", "kv", "head"),
        P("dp", "kv", "head"),
        P("dp", "kv", "head"),
        P("dp", "kv", "head"),
        P(),
    )
    out_specs = (P("dp", "head", "kv"), P("head"))
    return jax.shard_map(
        per_device, mesh=mesh, in_specs=in_specs, out_specs=out_specs, check_vma=False
    )
```

profile of v0, /device:TPU:0, one launch (start us, length us, event | category | flops | bytes accessed | tf_op | source)
XLA Modules:
  0.0 131.6 jit_solution(168695083922571773)
XLA Ops:
  7.2 2.3 %copy.18 = bf16[1,256,1792]{1,2,0:T(8,128)(2,1)} copy(bf16[1,256,1792]{2,1,0:T(8,128)(2,1)} %param.7) | data formatting | bytes 1835008 | tf_op args[0]
  9.6 1.0 copy.17
  10.6 7.2 %all_gather.12 = bf16[1,256,512]{1,2,0:T(8,128)(2,1)} all-gather(bf16[1,256,256]{1,2,0:T(8,128)(2,1)S(1)} %copy.17), channel_id=1, replica_groups=mesh['dp'=4,'head'=2,'kv'=4] {'head'}, dimensions={2}, use_global_device_ids=true | all-gather | bytes 393216 | tf_op jit(solution)/shard_map/all_gather | solution.py:114
  17.9 0.6 slice.3
  21.0 0.2 copy.21
  21.2 0.3 copy.22
  21.5 14.4 %all_gather.15 = bf16[1,1024,128]{2,1,0:T(8,128)(2,1)S(1)} all-gather(bf16[1,256,128]{2,1,0:T(8,128)(2,1)S(1)} %copy-done.2), channel_id=1, replica_groups=mesh['dp'=4,'head'=2,'kv'=4] {'kv'}, dimensions={1}, use_global_device_ids=true | all-gather | bytes 327680 | tf_op jit(solution)/shard_map/all_gather | solution.py:131
  35.9 6.6 %all-gather.5.cloned.1.call-done = bf16[1,256,3584]{1,2,0:T(8,128)(2,1)} async-done(((bf16[1,256,1792]{1,2,0:T(8,128)(2,1)}), bf16[1,256,3584]{1,2,0:T(8,128)(2,1)}) %all-gather.5.cloned.1.call-update) | async-done | bytes 1835024 | tf_op jit(solution)/shard_map/all_gather | solution.py:113
  42.5 2.9 %copy.20 = bf16[256,28,128]{2,0,1:T(8,128)(2,1)S(1)} copy(bf16[256,28,128]{0,2,1:T(8,128)(2,1)} %bitcast.99) | data formatting | bytes 3670016 | tf_op jit(solution)/shard_map/reshape | solution.py:119
  45.4 0.7 gather_fusion.1
  46.2 1.1 bitcast_select_fusion.1
  47.3 26.8 %all-gather.3.cloned.1.call-done = bf16[1,1024,512]{1,2,0:T(8,128)(2,1)} async-done(((bf16[1,256,512]{1,2,0:T(8,128)(2,1)}), bf16[1,1024,512]{1,2,0:T(8,128)(2,1)}) %all-gather.3.cloned.1.call-update) | async-done | bytes 1048592 | tf_op jit(solution)/shard_map/all_gather | solution.py:130
  74.1 9.4 %while.19 = (s32[]{:T(128)}, f32[1,14,256]{2,1,0:T(8,128)S(1)}, f32[1,14,256]{2,1,0:T(8,128)S(1)}, f32[1,14,256]{2,1,0:T(8,128)S(1)}, f32[1,7,256]{2,1,0:T(8,128...) while((s32[]{:T(128)}, f32[1,14,256]{2,1,0:T(8,128)S(1)}, ...), condition=%wide.region_6.7_spmd.clone, body=%wide.region_0.6_spmd.clone.sunk | while | flops 732774400 | bytes 36064820 | solution.py:74
  74.1 1.1 constant_dynamic-slice_fusion.3
  75.2 0.3 copy.24
  75.5 0.9 gather_fusion
  76.4 0.1 broadcast_compare_fusion.2
  76.6 2.6 %fusion.28 = (f32[14,256]{1,0:T(8,128)S(1)}, f32[14,512,256]{2,1,0:T(8,128)S(1)}) fusion(pred[256,512]{0,1:T(8,128)(4,1)S(1)} %broadcast_compare_fusion.2, bf16[1,256,14,128]{3,1,2,0:T(8,128)(2,1)} %get-tuple-element.346, bf16[14,512,128]{2,1,0:T(8,128)(2,1)S(1)} %gather_fusion, pred[14]{0:T(512)(128)(4,1)S(1)} %compare_and_fusion.5), kind=kOutput, calls=%fused_computation.9.clone.1 | convolution fusion | flops 476180992 | bytes 10237966 | tf_op jit(solution)/shard_map/while/body/bqpd,bkpd->bpqk/dot_general | solution.py:48
  79.3 0.8 select_reduce_fusion.4
  80.1 2.6 %fusion.29 = (f32[14,256]{1,0:T(8,128)S(1)}, f32[14,256]{1,0:T(8,128)S(1)}) fusion(f32[14,512,256]{2,1,0:T(8,128)S(1)} %get-tuple-element.292, f32[7,256,512]{1,2,0:T(8,128)S(1)} %get-tuple-element.293, f32[14,256]{1,0:T(8,128)S(1)} %bitcast.97, pred[256,512]{0,1:T(8,128)(4,1)S(1)} %broadcast_compare_fusion.2), kind=kLoop, calls=%fused_computation.6.clone.1 | loop fusion | flops 14672896 | bytes 11184128 | tf_op jit(solution)/shard_map/while/body/reduce_sum | solution.py:71
  82.7 0.8 select_reduce_fusion.5
  83.9 0.6 reduce_sum.61
  84.5 39.7 %psum.7 = f32[7]{0:T(128)S(1)} all-reduce(f32[7]{0:T(128)S(1)} %reduce_sum.64), channel_id=1, replica_groups=mesh['dp'=4,'head'=2,'kv'=4] {'dp','kv'}, use_global_device_ids=true, to_apply=%region_10.11 | all-reduce | flops 7 | bytes 56 | tf_op jit(solution)/shard_map/psum | solution.py:138
  124.3 0.5 broadcast_multiply_fusion
  (45 shorter events, 1.0 us)
Async XLA Ops:
  7.2 12.9 %copy-start = (s32[14,2]{0,1:T(2,128)S(1)}, s32[14,2]{0,1:T(2,128)}, u32[]{:S(2)}) copy-start(s32[14,2]{0,1:T(2,128)} %param.11) | copy-start | bytes 340
  7.2 13.8 %copy-start.1 = (bf16[1,256,896]{2,1,0:T(8,128)(2,1)S(1)}, bf16[1,256,896]{2,1,0:T(8,128)(2,1)}, u32[]{:S(2)}) copy-start(bf16[1,256,896]{2,1,0:T(8,128)(2,1)} %param.9) | copy-start | bytes 1376260
  7.2 14.3 %copy-start.2 = (bf16[1,256,128]{2,1,0:T(8,128)(2,1)S(1)}, bf16[1,256,128]{2,1,0:T(8,128)(2,1)}, u32[]{:S(2)}) copy-start(bf16[1,256,128]{2,1,0:T(8,128)(2,1)} %param.10) | copy-start | bytes 196612
  7.2 35.3 %all-gather.5.cloned.1.call-start = ((), (), s32[]{:S(2)}) async-start(), calls=%async_computation.1 | async-start | bytes 2752512 | tf_op jit(solution)/shard_map/all_gather | solution.py:113
  9.5 64.5 %all-gather.3.cloned.1.call-start = ((), (), s32[]{:S(2)}) async-start(), calls=%async_computation | async-start | bytes 1310720 | tf_op jit(solution)/shard_map/all_gather | solution.py:130
Sparse Core Ops, SparseCore 0:
  9.7 32.8 all-gather.4
  44.1 29.9 all-gather.2
where the time goes:
time: 132 us
  blocking collectives  61.4 us (47%)
  waiting for transfers between devices  33.5 us (25%)
  between operations  16.4 us (12%)
  local copies, waits for them, and re-layouts  11.3 us (9%)
  other arithmetic  5.49 us (4%)
  matrix products  3.37 us (3%)
    psum x1, blocking collectives, per_device(): total = lax.psum(head_sums, ('dp', 'kv'))  39.7 us
    all_gather x1, waiting for transfers between devices, per_device(): lax.all_gather(all_tk, 'kv', axis=1, tiled=True)  26.8 us
    all_gather x1, blocking collectives, per_device(): lax.all_gather(student_key, 'kv', axis=1, tiled=True)  14.4 us
    all_gather x1, blocking collectives, per_device(): lax.all_gather(teacher_key, 'head', axis=2, tiled=True)  7.22 us
    all_gather x1, waiting for transfers between devices, per_device(): lax.all_gather(teacher_query, 'head', axis=2, tiled=True)  6.6 us
    unnamed x10, local copies, waits for them, and re-layouts  3.76 us
    reshape x1, local copies, waits for them, and re-layouts, per_device(): all_tq.reshape(seq_dev, row_count, HT, DH)  2.89 us
  transfers between devices with their start and end apart: 2, of which 2 were waited for; matrix products, arithmetic and copies ran while one was open for 5% of the time, Pallas kernels for 0%

commit v1 on v0

--- a/solution.py
+++ b/solution.py
@@ -135,7 +135,8 @@
     pair_kl = finish_pairs(state, 2)
     kl_local = jnp.sum(pair_kl.reshape(seq_dev, local_student, 2, row_count), axis=2)
     head_sums = jnp.sum(kl_local, axis=(0, 2))
-    total = lax.psum(head_sums, ("dp", "kv"))
+    parts = lax.all_gather(head_sums, ("dp", "kv"))
+    total = jnp.sum(parts, axis=0)
     head_loss = total / (seq_dev * n_data * row_count * n_kv)
     return (kl_local, head_loss)
 

time: 132 us -> 132 us (level)
  waiting for transfers between devices: 33.5 us -> 32.1 us
    unnamed x0 -> x1, blocking collectives: none -> 39.7 us
    psum x1 -> x0, blocking collectives: 39.7 us -> none  [per_device(): total = lax.psum(head_sums, ('dp', 'kv'))]
    all_gather x1, waiting for transfers between devices: 6.6 us -> 5.26 us  [per_device(): lax.all_gather(teacher_query, 'head', axis=2, tiled=True)]
    unnamed x10 -> x15, local copies, waits for them, and re-layouts: 3.76 us -> 4.66 us
  transfers between devices with their start and end apart: 2 -> 2, of which waited for: 2 -> 2; matrix products, arithmetic and copies ran while one was open for 5% -> 6% of each run, Pallas kernels for 0% -> 0%
where the time goes in v1:
time: 132 us
  blocking collectives  61.4 us (47%)
  waiting for transfers between devices  32.1 us (24%)
  between operations  17.1 us (13%)
  local copies, waits for them, and re-layouts  12.2 us (9%)
  other arithmetic  5.52 us (4%)
  matrix products  3.37 us (3%)
    unnamed x1, blocking collectives  39.7 us
    all_gather x1, waiting for transfers between devices, per_device(): lax.all_gather(all_tk, 'kv', axis=1, tiled=True)  26.8 us
    all_gather x1, blocking collectives, per_device(): lax.all_gather(student_key, 'kv', axis=1, tiled=True)  14.4 us
    all_gather x1, blocking collectives, per_device(): lax.all_gather(teacher_key, 'head', axis=2, tiled=True)  7.22 us
    all_gather x1, waiting for transfers between devices, per_device(): lax.all_gather(teacher_query, 'head', axis=2, tiled=True)  5.26 us
    unnamed x15, local copies, waits for them, and re-layouts  4.66 us
    reshape x1, local copies, waits for them, and re-layouts, per_device(): all_tq.reshape(seq_dev, row_count, HT, DH)  2.89 us
  transfers between devices with their start and end apart: 2, of which 2 were waited for; matrix products, arithmetic and copies ran while one was open for 6% of the time, Pallas kernels for 0%

profile of v1, /device:TPU:0, one launch (start us, length us, event | category | flops | bytes accessed | tf_op | source)
XLA Modules:
  0.0 132.0 jit_solution(9095631313219517594)
XLA Ops:
  7.3 2.3 %copy.18 = bf16[1,256,1792]{1,2,0:T(8,128)(2,1)} copy(bf16[1,256,1792]{2,1,0:T(8,128)(2,1)} %param.7) | data formatting | bytes 1835008 | tf_op args[0]
  9.6 1.0 copy.17
  10.6 7.2 %all_gather.18 = bf16[1,256,512]{1,2,0:T(8,128)(2,1)} all-gather(bf16[1,256,256]{1,2,0:T(8,128)(2,1)S(1)} %copy.17), channel_id=1, replica_groups=mesh['dp'=4,'head'=2,'kv'=4] {'head'}, dimensions={2}, use_global_device_ids=true | all-gather | bytes 393216 | tf_op jit(solution)/shard_map/all_gather | solution.py:114
  17.9 0.6 slice.3
  21.2 0.3 copy.22
  21.5 0.6 dynamic-slice
  22.9 14.4 %all_gather.21 = bf16[1,1024,128]{2,1,0:T(8,128)(2,1)S(1)} all-gather(bf16[1,256,128]{2,1,0:T(8,128)(2,1)S(1)} %copy-done.2), channel_id=1, replica_groups=mesh['dp'=4,'head'=2,'kv'=4] {'kv'}, dimensions={1}, use_global_device_ids=true | all-gather | bytes 327680 | tf_op jit(solution)/shard_map/all_gather | solution.py:131
  37.3 5.3 %all-gather.6.cloned.1.call-done = bf16[1,256,3584]{1,2,0:T(8,128)(2,1)} async-done(((bf16[1,256,1792]{1,2,0:T(8,128)(2,1)}), bf16[1,256,3584]{1,2,0:T(8,128)(2,1)}) %all-gather.6.cloned.1.call-update) | async-done | bytes 1835024 | tf_op jit(solution)/shard_map/all_gather | solution.py:113
  42.6 2.9 %copy.20 = bf16[256,28,128]{2,0,1:T(8,128)(2,1)S(1)} copy(bf16[256,28,128]{0,2,1:T(8,128)(2,1)} %bitcast.100) | data formatting | bytes 3670016 | tf_op jit(solution)/shard_map/reshape | solution.py:119
  45.5 0.7 gather_fusion.1
  46.2 1.1 bitcast_select_fusion.1
  47.3 26.8 %all-gather.4.cloned.1.call-done = bf16[1,1024,512]{1,2,0:T(8,128)(2,1)} async-done(((bf16[1,256,512]{1,2,0:T(8,128)(2,1)}), bf16[1,1024,512]{1,2,0:T(8,128)(2,1)}) %all-gather.4.cloned.1.call-update) | async-done | bytes 1048592 | tf_op jit(solution)/shard_map/all_gather | solution.py:130
  74.1 9.4 %while.19 = (s32[]{:T(128)}, f32[1,14,256]{2,1,0:T(8,128)S(1)}, f32[1,14,256]{2,1,0:T(8,128)S(1)}, f32[1,14,256]{2,1,0:T(8,128)S(1)}, f32[1,7,256]{2,1,0:T(8,128...) while((s32[]{:T(128)}, f32[1,14,256]{2,1,0:T(8,128)S(1)}, ...), condition=%wide.region_6.7_spmd.clone, body=%wide.region_0.6_spmd.clone.sunk | while | flops 732774400 | bytes 36064820 | solution.py:74
  74.1 1.1 constant_dynamic-slice_fusion.3
  75.2 0.3 copy.24
  75.5 0.9 gather_fusion
  76.6 2.6 %fusion.28 = (f32[14,256]{1,0:T(8,128)S(1)}, f32[14,512,256]{2,1,0:T(8,128)S(1)}) fusion(pred[256,512]{0,1:T(8,128)(4,1)S(1)} %broadcast_compare_fusion.2, bf16[1,256,14,128]{3,1,2,0:T(8,128)(2,1)} %get-tuple-element.346, bf16[14,512,128]{2,1,0:T(8,128)(2,1)S(1)} %gather_fusion, pred[14]{0:T(512)(128)(4,1)S(1)} %compare_and_fusion.5), kind=kOutput, calls=%fused_computation.9.clone.1 | convolution fusion | flops 476180992 | bytes 10237966 | tf_op jit(solution)/shard_map/while/body/bqpd,bkpd->bpqk/dot_general | solution.py:48
  79.3 0.8 select_reduce_fusion.4
  80.1 2.6 %fusion.29 = (f32[14,256]{1,0:T(8,128)S(1)}, f32[14,256]{1,0:T(8,128)S(1)}) fusion(f32[14,512,256]{2,1,0:T(8,128)S(1)} %get-tuple-element.292, f32[7,256,512]{1,2,0:T(8,128)S(1)} %get-tuple-element.293, f32[14,256]{1,0:T(8,128)S(1)} %bitcast.98, pred[256,512]{0,1:T(8,128)(4,1)S(1)} %broadcast_compare_fusion.2), kind=kLoop, calls=%fused_computation.6.clone.1 | loop fusion | flops 14672896 | bytes 11184128 | tf_op jit(solution)/shard_map/while/body/reduce_sum | solution.py:71
  82.7 0.8 select_reduce_fusion.5
  83.7 0.6 reduce_sum.70
  84.5 0.2 dynamic-update-slice
  84.8 39.7 %all-reduce = f32[112]{0:T(128)S(1)} all-reduce(f32[112]{0:T(128)S(1)} %dynamic-update-slice), channel_id=2, replica_groups=mesh['dp'=4,'head'=2,'kv'=4] {'dp','kv'}, use_global_device_ids=true, to_apply=%add | all-reduce | flops 112 | bytes 896
  124.6 0.5 broadcast_multiply_fusion
  (52 shorter events, 1.5 us)
Async XLA Ops:
  7.2 12.9 %copy-start = (s32[14,2]{0,1:T(2,128)S(1)}, s32[14,2]{0,1:T(2,128)}, u32[]{:S(2)}) copy-start(s32[14,2]{0,1:T(2,128)} %param.11) | copy-start | bytes 340
  7.2 14.3 %copy-start.3 = (u32[32]{0:T(128)S(1)}, u32[32]{0:T(128)}, u32[]{:S(2)}) copy-start(u32[32]{0:T(128)} %constant.119) | copy-start | bytes 388
  7.2 13.8 %copy-start.1 = (bf16[1,256,896]{2,1,0:T(8,128)(2,1)S(1)}, bf16[1,256,896]{2,1,0:T(8,128)(2,1)}, u32[]{:S(2)}) copy-start(bf16[1,256,896]{2,1,0:T(8,128)(2,1)} %param.9) | copy-start | bytes 1376260
  7.2 15.6 %copy-start.2 = (bf16[1,256,128]{2,1,0:T(8,128)(2,1)S(1)}, bf16[1,256,128]{2,1,0:T(8,128)(2,1)}, u32[]{:S(2)}) copy-start(bf16[1,256,128]{2,1,0:T(8,128)(2,1)} %param.10) | copy-start | bytes 196612
  7.2 35.3 %all-gather.6.cloned.1.call-start = ((), (), s32[]{:S(2)}) async-start(), calls=%async_computation.1 | async-start | bytes 2752512 | tf_op jit(solution)/shard_map/all_gather | solution.py:113
  9.5 64.5 %all-gather.4.cloned.1.call-start = ((), (), s32[]{:S(2)}) async-start(), calls=%async_computation | async-start | bytes 1310720 | tf_op jit(solution)/shard_map/all_gather | solution.py:130
Sparse Core Ops, SparseCore 0:
  9.7 32.8 all-gather.5
  44.1 29.9 all-gather.3
